TPU v7x, 32 devices: a whole 2x2x4 slice. The times are simulated.
32 devices in a mesh: dp: 4 (over x, y), tp: 8 (over z, core).
Axes of the slice: x: 2, y: 2, z: 4, core: 2. Of those that a mesh axis runs over, the one named last changes fastest.
Arguments:
- x: bfloat16 [256, 5120], P('dp'), parts along dimension 0
- k_cache: bfloat16 [256, 4096, 8, 128], P('dp', None, 'tp'), parts along dimension 0
- v_cache: bfloat16 [256, 4096, 8, 128], P('dp', None, 'tp'), parts along dimension 0
- gain_a: bfloat16 [5120], replicated
- wq: bfloat16 [5120, 4096], P(None, 'tp')
- wo: bfloat16 [4096, 5120], P('tp')
- gain_m: bfloat16 [5120], replicated
- w_gate: bfloat16 [5120, 32768], P(None, 'tp')
- w_up: bfloat16 [5120, 32768], P(None, 'tp')
- w_down: bfloat16 [32768, 5120], P('tp')
Outputs:
- output: bfloat16 [256, 5120], P('dp'), parts along dimension 0
There are 4 independent parts. A program takes and returns all parts, laid end to end along the dimension named above; an argument that names none is the same for every part.
All inputs are finite; a program needn't handle non-finite values.
Results may differ from a plain program's by a relative error of at most 0.017.
Values are sent between devices in bfloat16 or wider.
A program may use at most 2 GiB of HBM per device.

v0:
```python
import jax
import jax.numpy as jnp
from jax import lax
from jax.sharding import PartitionSpec as P

HEAD = 128
THETA = 10000


def normed(x, gain):
    wide = x.astype(jnp.float32)
    scale = lax.rsqrt(jnp.mean(wide * wide, -1, keepdims=True) + 1e-6)
    return (wide * scale * gain.astype(jnp.float32)).astype(jnp.bfloat16)


def turned(t, place, theta):
    half = t.shape[-1] // 2
    angle = place.astype(jnp.float32)[:, None] * theta ** (-jnp.arange(half, dtype=jnp.float32) / half)
    cos, sin = jnp.cos(angle)[:, None], jnp.sin(angle)[:, None]
    a, b = t[..., :half].astype(jnp.float32), t[..., half:].astype(jnp.float32)
    return jnp.concatenate([a * cos - b * sin, b * cos + a * sin], -1).astype(jnp.bfloat16)


def matmul(a, w):
    return jnp.dot(a, w, preferred_element_type=jnp.float32).astype(jnp.bfloat16)


def einsum(form, a, b):
    return jnp.einsum(form, a.astype(jnp.float32), b.astype(jnp.float32))


def seen_by(a, wq, k_cache, v_cache, head, theta):
    batch, cache, kv_heads = k_cache.shape[:3]
    place = jnp.full((batch,), cache - 1)
    q = turned(matmul(a, wq).reshape(batch, -1, head), place, theta).reshape(batch, kv_heads, -1, head)
    scores = einsum("bgsd,bugd->bgsu", q, k_cache) * head**-0.5
    weights = jax.nn.softmax(scores, -1).astype(jnp.bfloat16)
    return einsum("bgsu,bugd->bgsd", weights, v_cache).astype(jnp.bfloat16).reshape(batch, -1)


def hidden_of(b, w_gate, w_up):
    gate = jnp.dot(b, w_gate, preferred_element_type=jnp.float32)
    up = jnp.dot(b, w_up, preferred_element_type=jnp.float32)
    return (jax.nn.silu(gate) * up).astype(jnp.bfloat16)


def solution(mesh):
    def added(t, term):
        return (t.astype(jnp.float32) + lax.psum(term.astype(jnp.bfloat16), "tp").astype(jnp.float32)).astype(jnp.bfloat16)

    def step(x, k_cache, v_cache, gain_a, wq, wo, gain_m, w_gate, w_up, w_down):
        seen = seen_by(normed(x, gain_a), wq, k_cache, v_cache, HEAD, THETA)
        h = added(x, jnp.dot(seen, wo, preferred_element_type=jnp.float32))
        return added(h, jnp.dot(hidden_of(normed(h, gain_m), w_gate, w_up), w_down, preferred_element_type=jnp.float32))

    states, cache, columns, rows_of = P("dp", None), P("dp", None, "tp", None), P(None, "tp"), P("tp", None)
    return jax.shard_map(
        step,
        mesh=mesh,
        in_specs=(states, cache, cache, P(None), columns, rows_of, P(None), columns, columns, rows_of),
        out_specs=states,
        check_vma=False,
    )
```

profile of v0, /device:TPU:0, one launch (start us, length us, event | category | flops | bytes accessed | tf_op | source)
XLA Modules:
  0.0 246.5 jit_solution(13195292035716297359)
XLA Ops:
  6.5 0.0 all-reduce.3.cloned.1.call-start
  6.6 0.7 convert_element_type.66
  7.3 1.3 fusion.12
  8.6 3.8 %convolution_convert_fusion.2 = bf16[64,512]{1,0:T(8,128)(2,1)S(1)} fusion(bf16[5120,512]{1,0:T(8,128)(2,1)} %param.14, bf16[64,5120]{1,0:T(8,128)(2,1)} %param.10, f32[5120]{0:T(1024)S(1)} %convert_element_type.66, f32[64]{0:T(128)S(1)} %add_rsqrt_fusion.1), kind=kOutput, calls=%fused_computation.29 | convolution fusion | flops 336887808 | bytes 5984512 | tf_op jit(solution)/shard_map/dot_general | solution.py:25
  12.4 0.1 fusion.39
  12.6 0.1 pad_maximum_fusion
  12.7 27.7 %fusion.40 = (f32[64,4]{1,0:T(8,128)S(1)}, f32[64,4,4096]{2,1,0:T(4,128)}) fusion(bf16[64,4096,1,128]{3,1,2,0:T(8,128)(2,1)} %param.11, bf16[64,4,128]{2,0,1:T(8,128)(2,1)S(1)} %pad_maximum_fusion), kind=kOutput, calls=%fused_computation.51 | convolution fusion | flops 271585280 | bytes 71369728 | tf_op jit(solution)/shard_map/sub | solution.py:37
  40.4 23.9 %fusion.20 = bf16[64,4,128]{2,1,0:T(4,128)(2,1)S(1)} fusion(bf16[64,4096,1,128]{3,1,2,0:T(8,128)(2,1)} %param.12, f32[64,4,4096]{2,1,0:T(4,128)} %get-tuple-element.12, f32[64,4]{1,0:T(8,128)S(1)} %get-tuple-element.11), kind=kOutput, calls=%fused_computation.28 | convolution fusion | flops 270565376 | bytes 71369728 | tf_op jit(solution)/shard_map/bgsu,bugd->bgsd/dot_general | solution.py:29
  64.4 0.0 copy-start.1
  64.4 0.0 copy-start
  64.4 4.4 %convolution_convert_fusion.1 = bf16[64,5120]{1,0:T(8,128)(2,1)} fusion(bf16[512,5120]{1,0:T(8,128)(2,1)} %param.15, bf16[8,8,4,128]{3,2,1,0:T(4,128)(2,1)S(1)} %bitcast.22), kind=kOutput, calls=%fused_computation.7 | convolution fusion | flops 335872000 | bytes 5963776 | tf_op jit(solution)/shard_map/dot_general | solution.py:53
  68.8 0.0 all-reduce.3.cloned.1.call-update
  68.9 0.2 all-reduce.5.cloned.1.call-start
  69.1 0.0 copy-done.1
  69.1 59.5 %all-reduce.3.cloned.1.call-done = bf16[64,5120]{1,0:T(8,128)(2,1)} async-done(((bf16[64,5120]{1,0:T(8,128)(2,1)}), bf16[64,5120]{1,0:T(8,128)(2,1)}) %all-reduce.3.cloned.1.call-update) | async-done | bytes 655376 | tf_op jit(solution)/shard_map/psum | solution.py:49
  128.6 0.0 copy-done
  128.6 1.4 fusion.16
  130.1 16.8 %fusion.27 = f32[64,4096]{1,0:T(8,128)S(1)} fusion(bf16[5120,4096]{1,0:T(8,128)(2,1)} %param.17, bf16[64,5120]{1,0:T(8,128)(2,1)S(1)} %get-tuple-element.6, f32[5120]{0:T(1024)S(1)} %convert_element_type.77, f32[64]{0:T(128)S(1)} %add_rsqrt_fusion), kind=kOutput, calls=%fused_computation.32 | convolution fusion | flops 2685665280 | bytes 43667712 | tf_op jit(solution)/shard_map/dot_general | solution.py:42
  146.9 17.1 %fusion.10 = bf16[64,4096]{1,0:T(8,128)(2,1)S(1)} fusion(bf16[5120,4096]{1,0:T(8,128)(2,1)} %param.18, f32[64,4096]{1,0:T(8,128)S(1)} %fusion.27, bf16[64,5120]{1,0:T(8,128)(2,1)S(1)} %get-tuple-element.6, f32[5120]{0:T(1024)S(1)} %convert_element_type.77, f32[64]{0:T(128)S(1)} %add_rsqrt_fusion), kind=kOutput, calls=%fused_computation.11 | convolution fusion | flops 2687238144 | bytes 44192000 | tf_op jit(solution)/shard_map/dot_general | solution.py:43
  164.0 17.6 %convolution_convert_fusion = bf16[64,5120]{1,0:T(8,128)(2,1)} fusion(bf16[64,4096]{1,0:T(8,128)(2,1)S(1)} %fusion.10, bf16[4096,5120]{1,0:T(8,128)(2,1)} %param.19), kind=kOutput, calls=%fused_computation.6 | convolution fusion | flops 2684682240 | bytes 43122688 | tf_op jit(solution)/shard_map/dot_general | solution.py:54
  181.6 0.0 all-reduce.5.cloned.1.call-update
  181.6 56.0 %all-reduce.5.cloned.1.call-done = bf16[64,5120]{1,0:T(8,128)(2,1)} async-done(((bf16[64,5120]{1,0:T(8,128)(2,1)}), bf16[64,5120]{1,0:T(8,128)(2,1)}) %all-reduce.5.cloned.1.call-update) | async-done | bytes 655376 | tf_op jit(solution)/shard_map/psum | solution.py:49
  237.6 2.1 fusion.19
  (6 shorter events, 0.1 us)
Async XLA Ops:
  6.5 122.1 %all-reduce.3.cloned.1.call-start = ((), (), s32[]{:S(2)}) async-start(), calls=%async_computation | async-start | bytes 1310720 | tf_op jit(solution)/shard_map/psum | solution.py:49
  64.4 4.7 %copy-start.1 = (bf16[5120]{0:T(1024)(128)(2,1)S(1)}, bf16[5120]{0:T(1024)(128)(2,1)}, u32[]{:S(2)}) copy-start(bf16[5120]{0:T(1024)(128)(2,1)} %param.16) | copy-start | bytes 30724
  64.4 64.2 %copy-start = (bf16[64,5120]{1,0:T(8,128)(2,1)S(1)}, bf16[64,5120]{1,0:T(8,128)(2,1)}, u32[]{:S(2)}) copy-start(bf16[64,5120]{1,0:T(8,128)(2,1)} %param.10) | copy-start | bytes 1966084
  68.9 168.8 %all-reduce.5.cloned.1.call-start = ((), (), s32[]{:S(2)}) async-start(), calls=%async_computation.1 | async-start | bytes 1310720 | tf_op jit(solution)/shard_map/psum | solution.py:49
Sparse Core Ops, SparseCore 0:
  69.0 59.6 all-reduce.2
  181.7 55.8 all-reduce.4
where the time goes:
time: 247 us
  waiting for transfers between devices  116 us (47%)
  matrix products  111 us (45%)
  between operations  13.5 us (5%)
  other arithmetic  5.72 us (2%)
    psum x2, waiting for transfers between devices, added(): lax.psum(term.astype(jnp.bfloat16), 'tp').astype(jnp.float32)  116 us
    sub x1, matrix products, seen_by(): weights = jax.nn.softmax(scores, -1).astype(jnp.bfloat16)  27.7 us
    dot_general x1, matrix products, einsum(): return jnp.einsum(form, a.astype(jnp.float32), b.astype(jnp.float32))  23.9 us
    dot_general x1, matrix products, step(): jnp.dot(hidden_of(normed(h, gain_m), w_gate, w_up), w_down, preferred_ele...  17.6 us
    dot_general x1, matrix products, hidden_of(): up = jnp.dot(b, w_up, preferred_element_type=jnp.float32)  17.1 us
    dot_general x1, matrix products, hidden_of(): gate = jnp.dot(b, w_gate, preferred_element_type=jnp.float32)  16.8 us
  transfers between devices with their start and end apart: 2, of which 2 were waited for; matrix products, arithmetic and copies ran while one was open for 0% of the time, Pallas kernels for 0%

commit v1 on v0

v1 whole, which is shorter than its diff:
```python
import functools

import jax
import jax.numpy as jnp
import numpy as np
from jax import lax
from jax.experimental import pallas as pl
from jax.experimental.pallas import tpu as pltpu
from jax.sharding import PartitionSpec as P

HEAD = 128
THETA = 10000
MESH = pl.DeviceIdType.MESH
F32, BF16 = jnp.float32, jnp.bfloat16

CORES = 2
LINE = 4
SEQS = 4
KV_SLOTS = 3
W_SLOTS = 6
WIDE = 256
ROWS = 16


def kernel(
    x_hbm, k_hbm, v_hbm, gain_a_ref, wq_hbm, wo_hbm, gain_m_ref, w_gate_hbm, w_up_hbm, w_down_hbm, turn_ref,
    y_hbm,
    x_ref, normed_ref, h_ref, y_ref, hidden_ref, q_ref, seen_ref, kv_ref, w_ref,
    own1, pair_out1, pair_in1, line_out1, line_in1,
    own2, pair_out2, pair_in2, line_out2, line_in2,
    x_sem, kv_sem, w_sem, wo_sem, y_sem, sum1_sem, sum2_sem,
):
    batch, cache, _ = k_hbm.shape
    d = x_hbm.shape[1]
    heads = wq_hbm.shape[1] // HEAD
    ff = w_gate_hbm.shape[1]
    half_cache = cache // 2
    half_d, part_d = d // CORES, d // (CORES * LINE)
    row_part = batch // LINE
    steps = batch // SEQS
    chunks = batch // ROWS
    per_chunk = ROWS // SEQS
    ups = ff // WIDE
    downs = d // (2 * WIDE)
    q_blocks = heads * HEAD // WIDE
    wo_blocks = half_d // WIDE
    wo_rows = wo_hbm.shape[0]

    me = lax.axis_index("tp")
    core = lax.rem(me, CORES)
    z = me // CORES
    partner = z * CORES + (1 - core)

    def at_z(r):
        return lax.rem(z + r, LINE)

    def peer(r):
        return at_z(r) * CORES + core

    def aligned(i, m):
        return pl.multiple_of(i, m)

    def kv_copies(i, slot):
        rows = pl.ds(aligned(i * SEQS, SEQS), SEQS)
        return [
            pltpu.make_async_copy(hbm.at[rows], kv_ref.at[slot, which], kv_sem.at[slot, which])
            for which, hbm in enumerate((k_hbm, v_hbm))
        ]

    def wq_copies():
        return [
            pltpu.make_async_copy(wq_hbm.at[:, pl.ds(n * WIDE, WIDE)], w_ref.at[0, n, pl.ds(0, d)], w_sem.at[0, n]) for n in range(q_blocks)
        ]

    def wo_copies():
        return [
            pltpu.make_async_copy(
                wo_hbm.at[:, pl.ds((side * wo_blocks + n) * WIDE, WIDE)],
                w_ref.at[W_SLOTS - 1, side, pl.ds(n * wo_rows, wo_rows)],
                wo_sem.at[side, n],
            )
            for side in range(2)
            for n in range(wo_blocks)
        ]

    def up_copies(u, slot):
        columns = pl.ds(aligned(u * WIDE, WIDE), WIDE)
        return [
            pltpu.make_async_copy(hbm.at[:, columns], w_ref.at[slot, side, pl.ds(0, d)], w_sem.at[slot, side])
            for side, hbm in enumerate((w_gate_hbm, w_up_hbm))
        ]

    def down_copies(n, slot):
        return [
            pltpu.make_async_copy(
                w_down_hbm.at[:, pl.ds(aligned((2 * n + side) * WIDE, WIDE), WIDE)],
                w_ref.at[slot, side, pl.ds(0, ff)],
                w_sem.at[slot, side],
            )
            for side in range(2)
        ]

    def start(copies):
        for copy in copies:
            copy.start()

    def wait(copies):
        for copy in copies:
            copy.wait()

    def wait_recv(copies):
        for copy in copies:
            copy.wait_recv()

    def start_weights(u):
        slot = lax.rem(u, W_SLOTS)

        @pl.when(u < ups)
        def _():
            start(up_copies(u, slot))

        @pl.when((u >= ups) & (u < ups + downs))
        def _():
            start(down_copies(u - ups, slot))

    x_copy = pltpu.make_async_copy(x_hbm, x_ref, x_sem)
    x_copy.start()
    start(wq_copies())
    for i in range(KV_SLOTS):
        start(kv_copies(i, i))
    start(wo_copies())

    barrier = pltpu.get_barrier_semaphore()
    for other in [partner] + [peer(r) for r in range(1, LINE)]:
        pl.semaphore_signal(barrier, inc=1, device_id={"tp": other}, device_id_type=MESH)

    part = 512

    def norm_rows(src, rows, gain):
        count = rows.size
        total = jnp.zeros((count, 1), F32)
        for j in range(d // part):
            wide = src[rows, pl.ds(j * part, part)].astype(F32)
            total += jnp.sum(wide * wide, -1, keepdims=True)
        scale = lax.rsqrt(total / d + 1e-6)
        for j in range(d // part):
            columns = pl.ds(j * part, part)
            wide = src[rows, columns].astype(F32)
            normed_ref[rows, columns] = (wide * scale * gain[:, columns].astype(F32)).astype(BF16)

    x_copy.wait()
    for c in range(chunks):
        norm_rows(x_ref, pl.ds(c * ROWS, ROWS), gain_a_ref)
    wait(wq_copies())
    cos, sin = turn_ref[0:1, :], turn_ref[1:2, :]
    q_ref[...] = jnp.zeros_like(q_ref)
    a = normed_ref[...]
    for n in range(q_blocks):
        q = jnp.dot(a, w_ref[0, n, 0:d], preferred_element_type=F32).astype(BF16).astype(F32)
        for j in range(WIDE // HEAD):
            head = n * (WIDE // HEAD) + j
            t = q[:, j * HEAD : (j + 1) * HEAD]
            t = (t * cos + pltpu.roll(t, HEAD // 2, 1) * sin).astype(BF16).astype(F32)
            q_ref[0, pl.ds(head, batch, stride=2 * heads), :] = t
            q_ref[1, pl.ds(heads + head, batch, stride=2 * heads), :] = t

    pl.semaphore_wait(barrier, LINE)

    def remote(src, dst, send, recv, other):
        return pltpu.make_async_remote_copy(
            src_ref=src, dst_ref=dst, send_sem=send, recv_sem=recv, device_id={"tp": other}, device_id_type=MESH
        )

    class Sum:
        def __init__(self, c, sems, pair_out, pair_in, line_out, line_in, part_of, block_of):
            def one(src, dst, place, other):
                return remote(src, dst, sems.at[c, 0, place], sems.at[c, 1, place], other)

            def gathered(place, n, other):
                return one(block_of(place), block_of(place), n, other)

            steps = range(1, LINE)
            self.pair = lambda: [one(pair_out.at[c], pair_in.at[c], 0, partner)]
            self.line = lambda: [one(part_of(line_out, at_z(r)), line_in.at[c, r - 1], r, peer(r)) for r in steps]
            self.gather = lambda: [gathered(z, 3 + r, peer(r)) for r in steps]
            self.own = lambda: [gathered(z, 7, partner)]
            self.passed = lambda: [gathered(at_z(LINE - r), 7 + r, partner) for r in steps]

        def send_pair(self):
            start(self.pair())

        def send_line(self, add_pair):
            wait_recv(self.pair())
            add_pair()
            start(self.line())

        def send_gather(self, add_line):
            wait_recv(self.line())
            add_line()
            start(self.gather() + self.own())

        def pass_on(self):
            for got, copy in zip(self.gather(), self.passed()):
                got.wait_recv()
                copy.start()

        def finish(self):
            wait_recv(self.own() + self.passed())
            for copy in self.pair() + self.line() + self.gather() + self.own() + self.passed():
                copy.wait_send()

    def sum1(c):
        rows = pl.ds(aligned(c * ROWS, ROWS), ROWS)

        def part_of(ref, place):
            return ref.at[c, :, pl.ds(aligned(place * part_d, part_d), part_d)]

        def block_of(place):
            return h_ref.at[rows, pl.ds(aligned(core * half_d + place * part_d, part_d), part_d)]

        return Sum(c, sum1_sem, pair_out1, pair_in1, line_out1, line_in1, part_of, block_of)

    def add_pair1(c):
        def add():
            for j in range(half_d // part):
                columns = pl.ds(j * part, part)
                line_out1[c, :, columns] = (own1[c, :, columns] + pair_in1[c, :, columns].astype(F32)).astype(BF16)

        return add

    def add_line1(c):
        def add():
            rows = pl.ds(aligned(c * ROWS, ROWS), ROWS)
            mine = pl.ds(aligned(z * part_d, part_d), part_d)
            columns = pl.ds(aligned(core * half_d + z * part_d, part_d), part_d)
            total = own1[c, :, mine] + pair_in1[c, :, mine].astype(F32)
            for r in range(LINE - 1):
                total += line_in1[c, r].astype(F32)
            h_ref[rows, columns] = (x_ref[rows, columns].astype(F32) + total).astype(BF16)

        return add

    scaling = HEAD**-0.5

    def attend(i, slot):
        for s in range(SEQS):
            at = pl.ds(aligned((i * SEQS + s) * 2 * heads, 2 * heads), 2 * heads)
            q = jnp.concatenate([q_ref[0, at, :], q_ref[1, at, :]], 1).astype(BF16)
            keys = jnp.concatenate([kv_ref[slot, 0, s, 0:half_cache], kv_ref[slot, 0, s, half_cache:cache]], 1)
            scores = lax.dot_general(q, keys, (((1,), (1,)), ((), ())), preferred_element_type=F32) * scaling
            top = jnp.max(scores, 1, keepdims=True)
            top = jnp.maximum(top, pltpu.roll(top, heads, 0))
            e = jnp.exp(scores - top)
            total = jnp.sum(e, 1, keepdims=True)
            total = total + pltpu.roll(total, heads, 0)
            weights = (e * (1.0 / total)).astype(BF16)
            values = jnp.concatenate([kv_ref[slot, 1, s, 0:half_cache], kv_ref[slot, 1, s, half_cache:cache]], 1)
            both = jnp.dot(weights, values, preferred_element_type=F32)
            seen_ref[at, :] = both[:, 0:HEAD] + pltpu.roll(both[:, HEAD : 2 * HEAD], heads, 0)

    def project(c):
        seen = jnp.concatenate(
            [seen_ref[pl.ds(c * ROWS * 2 * heads + head, ROWS, stride=2 * heads), :] for head in range(heads)], 1
        ).astype(BF16)
        slot = W_SLOTS - 1
        for n in range(wo_blocks):
            rows, columns = pl.ds(n * wo_rows, wo_rows), pl.ds(n * WIDE, WIDE)
            own1[c, :, columns] = jnp.dot(seen, w_ref[slot, core, rows], preferred_element_type=F32)
            pair_out1[c, :, columns] = jnp.dot(seen, w_ref[slot, 1 - core, rows], preferred_element_type=F32).astype(BF16)

    @pl.loop(0, steps)
    def _(i):
        slot = lax.rem(i, KV_SLOTS)
        c = i // per_chunk
        place = lax.rem(i, per_chunk)
        wait(kv_copies(i, slot))
        attend(i, slot)

        @pl.when(i + KV_SLOTS < steps)
        def _():
            start(kv_copies(i + KV_SLOTS, slot))

        @pl.when(i == steps - KV_SLOTS)
        def _():
            start_weights(0)

        @pl.when(i == steps - KV_SLOTS + 1)
        def _():
            start_weights(1)
            start_weights(2)

        @pl.when(i == steps - KV_SLOTS + 2)
        def _():
            for u in range(3, W_SLOTS - 1):
                start_weights(u)

        @pl.when((place == 0) & (i >= per_chunk))
        def _():
            sum1(c - 1).send_line(add_pair1(c - 1))

        @pl.when((place == 0) & (i >= 2 * per_chunk))
        def _():
            sum1(c - 2).pass_on()

        @pl.when((place == per_chunk - 2) & (i >= per_chunk))
        def _():
            sum1(c - 1).send_gather(add_line1(c - 1))

        @pl.when(place == per_chunk - 1)
        def _():
            @pl.when(i == per_chunk - 1)
            def _():
                wait(wo_copies())

            project(c)
            sum1(c).send_pair()

    start_weights(W_SLOTS - 1)
    last = chunks - 1
    sum1(last - 1).pass_on()
    sum1(last).send_line(add_pair1(last))

    @pl.loop(0, last)
    def _(c):
        sum1(c).finish()
        norm_rows(h_ref, pl.ds(aligned(c * ROWS, ROWS), ROWS), gain_m_ref)

    sum1(last).send_gather(add_line1(last))
    sum1(last).pass_on()
    sum1(last).finish()
    norm_rows(h_ref, pl.ds(last * ROWS, ROWS), gain_m_ref)

    @pl.loop(0, ups)
    def _(u):
        slot = lax.rem(u, W_SLOTS)
        wait(up_copies(u, slot))
        b = normed_ref[...]
        gate = jnp.dot(b, w_ref[slot, 0, 0:d], preferred_element_type=F32)
        up = jnp.dot(b, w_ref[slot, 1, 0:d], preferred_element_type=F32)
        hidden_ref[:, pl.ds(aligned(u * WIDE, WIDE), WIDE)] = (gate * (1.0 / (1.0 + jnp.exp(-gate))) * up).astype(BF16)
        start_weights(u + W_SLOTS)

    def sum2(n):
        def part_of(ref, place):
            return ref.at[n, pl.ds(aligned(place * row_part, row_part), row_part)]

        def block_of(place):
            columns = pl.ds(aligned((2 * n + core) * WIDE, WIDE), WIDE)
            return y_ref.at[pl.ds(aligned(place * row_part, row_part), row_part), columns]

        return Sum(n, sum2_sem, pair_out2, pair_in2, line_out2, line_in2, part_of, block_of)

    def add_pair2(n):
        def add():
            line_out2[n] = (own2[n] + pair_in2[n].astype(F32)).astype(BF16)

        return add

    def add_line2(n):
        def add():
            rows = pl.ds(aligned(z * row_part, row_part), row_part)
            columns = pl.ds(aligned((2 * n + core) * WIDE, WIDE), WIDE)
            total = own2[n, rows] + pair_in2[n, rows].astype(F32)
            for r in range(LINE - 1):
                total += line_in2[n, r].astype(F32)
            y_ref[rows, columns] = (h_ref[rows, columns].astype(F32) + total).astype(BF16)

        return add

    lag_line, lag_gather, lag_pass = 1, 4, 7

    @pl.loop(0, downs + lag_pass)
    def _(t):
        @pl.when(t < downs)
        def _():
            slot = lax.rem(ups + t, W_SLOTS)
            wait(down_copies(t, slot))
            hidden = hidden_ref[...]
            own2[t] = jnp.dot(hidden, w_ref[slot, core, 0:ff], preferred_element_type=F32)
            pair_out2[t] = jnp.dot(hidden, w_ref[slot, 1 - core, 0:ff], preferred_element_type=F32).astype(BF16)
            sum2(t).send_pair()
            start_weights(ups + t + W_SLOTS)

        @pl.when((t >= lag_line) & (t < downs + lag_line))
        def _():
            sum2(t - lag_line).send_line(add_pair2(t - lag_line))

        @pl.when((t >= lag_gather) & (t < downs + lag_gather))
        def _():
            sum2(t - lag_gather).send_gather(add_line2(t - lag_gather))

        @pl.when(t >= lag_pass)
        def _():
            sum2(t - lag_pass).pass_on()

    @pl.loop(0, downs)
    def _(n):
        sum2(n).finish()

    y_copy = pltpu.make_async_copy(y_ref, y_hbm, y_sem)
    y_copy.start()
    y_copy.wait()


def solution(mesh):
    def step(x, k_cache, v_cache, gain_a, wq, wo, gain_m, w_gate, w_up, w_down):
        batch, cache = k_cache.shape[:2]
        d, ff = x.shape[1], w_gate.shape[1]
        heads = wq.shape[1] // HEAD
        half_d, part_d, row_part = d // CORES, d // (CORES * LINE), batch // LINE
        chunks, downs = batch // ROWS, d // (2 * WIDE)
        half = HEAD // 2
        angle = (cache - 1) * float(THETA) ** (-np.arange(half) / half)
        cos, sin = np.cos(angle), np.sin(angle)
        turn = np.zeros((8, HEAD), np.float32)
        turn[0], turn[1] = np.concatenate([cos, cos]), np.concatenate([-sin, sin])
        anywhere, vmem = pl.BlockSpec(memory_space=pl.ANY), pl.BlockSpec(memory_space=pltpu.VMEM)
        dma = pltpu.SemaphoreType.DMA
        return pl.pallas_call(
            kernel,
            name="decoder_layer",
            out_shape=jax.ShapeDtypeStruct(x.shape, BF16),
            in_specs=[anywhere, anywhere, anywhere, vmem, anywhere, anywhere, vmem, anywhere, anywhere, anywhere, vmem],
            out_specs=anywhere,
            scratch_shapes=[
                pltpu.VMEM(x.shape, BF16),
                pltpu.VMEM(x.shape, BF16),
                pltpu.VMEM(x.shape, BF16),
                pltpu.VMEM(x.shape, BF16),
                pltpu.VMEM((batch, ff), BF16),
                pltpu.VMEM((2, batch * 2 * heads, HEAD), F32),
                pltpu.VMEM((batch * 2 * heads, HEAD), F32),
                pltpu.VMEM((KV_SLOTS, 2, SEQS, cache, HEAD), BF16),
                pltpu.VMEM((W_SLOTS, 2, max(d, ff), WIDE), BF16),
                pltpu.VMEM((chunks, ROWS, half_d), F32),
                pltpu.VMEM((chunks, ROWS, half_d), BF16),
                pltpu.VMEM((chunks, ROWS, half_d), BF16),
                pltpu.VMEM((chunks, ROWS, half_d), BF16),
                pltpu.VMEM((chunks, LINE - 1, ROWS, part_d), BF16),
                pltpu.VMEM((downs, batch, WIDE), F32),
                pltpu.VMEM((downs, batch, WIDE), BF16),
                pltpu.VMEM((downs, batch, WIDE), BF16),
                pltpu.VMEM((downs, batch, WIDE), BF16),
                pltpu.VMEM((downs, LINE - 1, row_part, WIDE), BF16),
                dma,
                dma((KV_SLOTS, 2)),
                dma((W_SLOTS, 2)),
                dma((2, half_d // WIDE)),
                dma,
                dma((chunks, 2, 11)),
                dma((downs, 2, 11)),
            ],
            compiler_params=pltpu.CompilerParams(collective_id=0, has_side_effects=True, vmem_limit_bytes=67043328),
        )(
            x,
            k_cache.reshape(batch, cache, HEAD),
            v_cache.reshape(batch, cache, HEAD),
            gain_a.reshape(1, d),
            wq,
            wo,
            gain_m.reshape(1, d),
            w_gate,
            w_up,
            w_down,
            jnp.asarray(turn),
        )

    states, cache, columns, rows_of = P("dp", None), P("dp", None, "tp", None), P(None, "tp"), P("tp", None)
    return jax.shard_map(
        step,
        mesh=mesh,
        in_specs=(states, cache, cache, P(None), columns, rows_of, P(None), columns, columns, rows_of),
        out_specs=states,
        check_vma=False,
    )
```

time: 247 us -> 133 us (0.54)
  Pallas kernels: 0 us -> 128 us
  waiting for transfers between devices: 116 us -> 0 us
  matrix products: 111 us -> 0 us
  between operations: 13.5 us -> 0.01 us
  other arithmetic: 5.72 us -> 0 us
  local copies, waits for them, and re-layouts: 0.14 us -> 4.6 us
    pallas_call x0 -> x1, Pallas kernels: none -> 128 us  [step(): pl.pallas_call(kernel, name='decoder_layer', out_shape=jax.ShapeDtypeStru...]
    psum x2 -> x0, waiting for transfers between devices: 116 us -> none  [added(): lax.psum(term.astype(jnp.bfloat16), 'tp').astype(jnp.float32)]
    dot_general x6 -> x0, matrix products: 83.6 us -> none  [the longest x1 23.9 us: einsum(): return jnp.einsum(form, a.astype(jnp.float32), b.astype(jnp.float32))]
    sub x1 -> x0, matrix products: 27.7 us -> none  [seen_by(): weights = jax.nn.softmax(scores, -1).astype(jnp.bfloat16)]
    convert_element_type x3 -> x0, other arithmetic: 2.79 us -> none  [the longest x1 2.07 us: added(): (t.astype(jnp.float32) + lax.psum(term.astype(jnp.bfloat16), 'tp').astype...]
    reduce_sum x2 -> x0, other arithmetic: 2.73 us -> none  [normed(): scale = lax.rsqrt(jnp.mean(wide * wide, -1, keepdims=True) + 1e-06)]
    reshape x1 -> x2, local copies, waits for them, and re-layouts: 0.02 us -> 2.63 us  [the longest x1 1.32 us: step(): gain_a.reshape(1, d)]
  transfers between devices with their start and end apart: 2 -> 0, of which waited for: 2 -> 0; matrix products, arithmetic and copies ran while one was open for 0% -> 0% of each run, Pallas kernels for 0% -> 0%
where the time goes in v1:
time: 133 us; the launch traced here: 132 us
  Pallas kernels  128 us (96%)
  local copies, waits for them, and re-layouts  4.6 us (3%)
    pallas_call x1, Pallas kernels, step(): pl.pallas_call(kernel, name='decoder_layer', out_shape=jax.ShapeDtypeStru...  128 us

profile of v1, /device:TPU:0, one launch (start us, length us, event | category | flops | bytes accessed | tf_op | source)
XLA Modules:
  0.0 132.3 jit_solution(9696715989042181216)
XLA Ops:
  0.0 1.3 reshape.14.gain_a_ref
  1.3 1.3 reshape.15.gain_m_ref
  2.6 127.7 %decoder_layer.1 = bf16[64,5120]{1,0:T(8,128)(2,1)} custom-call(bf16[64,5120]{1,0:T(8,128)(2,1)} %x_hbm.1, bf16[64,4096,128]{2,1,0:T(8,128)(2,1)} %bitcast.k_hbm, bf16[64,4096,128]{2,1,0:T(8,128)(2,1)} %bitcast.1.v_hbm, bf16[1,5120]{1,0:T(2,128)(2,1)} %reshape.14.gain_a_ref, bf16[5120,512]{1,0:T(8,128)(2,1)} %wq_hbm.1, bf16[512,5120]{1,0:T(8,128)(2,1)} %wo_hbm.1, ...), custom_call_target="tpu_custom_call" | custom-call | tf_op jit(solution)/shard_map/decoder_layer/pallas_call | solution.py:419
  130.4 2.0 %copy.13 = bf16[64,5120]{1,0:T(8,128)(2,1)} copy(bf16[64,5120]{1,0:T(8,128)(2,1)} %decoder_layer.1) | data formatting | bytes 1310720

commit v2 on v1

--- a/solution.py
+++ b/solution.py
@@ -16,22 +16,25 @@
 CORES = 2
 LINE = 4
 SEQS = 4
+KV_CUTS = 1
 KV_SLOTS = 3
+EARLY = KV_SLOTS
 W_SLOTS = 6
 WIDE = 256
+LAGS = 1, 5, 9, 12
 ROWS = 16
 
 
 def kernel(
     x_hbm, k_hbm, v_hbm, gain_a_ref, wq_hbm, wo_hbm, gain_m_ref, w_gate_hbm, w_up_hbm, w_down_hbm, turn_ref,
-    y_hbm,
-    x_ref, normed_ref, h_ref, y_ref, hidden_ref, q_ref, seen_ref, kv_ref, w_ref,
-    own1, pair_out1, pair_in1, line_out1, line_in1,
-    own2, pair_out2, pair_in2, line_out2, line_in2,
-    x_sem, kv_sem, w_sem, wo_sem, y_sem, sum1_sem, sum2_sem,
+    y_ref,
+    x_ref, normed_ref, h_ref, hidden_ref, q_ref, seen_ref, kv_ref, w_ref,
+    own1, pair_out1, pair_in1, line_in1,
+    own2, pair_out2, pair_in2, line_in2,
+    x_sem, kv_sem, w_sem, wo_sem, sum1_sem, sum2_sem,
 ):
-    batch, cache, _ = k_hbm.shape
-    d = x_hbm.shape[1]
+    batch, d = x_hbm.shape
+    cache = k_hbm.shape[0] // batch
     heads = wq_hbm.shape[1] // HEAD
     ff = w_gate_hbm.shape[1]
     half_cache = cache // 2
@@ -61,10 +64,27 @@
         return pl.multiple_of(i, m)
 
     def kv_copies(i, slot):
-        rows = pl.ds(aligned(i * SEQS, SEQS), SEQS)
+        part = SEQS * cache // KV_CUTS
         return [
-            pltpu.make_async_copy(hbm.at[rows], kv_ref.at[slot, which], kv_sem.at[slot, which])
+            pltpu.make_async_copy(
+                hbm.at[pl.ds(aligned((i * KV_CUTS + j) * part, part), part)],
+                kv_ref.at[slot, which, pl.ds(j * part, part)],
+                kv_sem.at[slot, which, j],
+            )
+            for j in range(KV_CUTS)
             for which, hbm in enumerate((k_hbm, v_hbm))
+        ]
+
+    def early_copies(u):
+        slot = lax.rem(u + steps - EARLY, KV_SLOTS)
+        return [
+            pltpu.make_async_copy(
+                hbm.at[:, pl.ds(aligned((2 * u + j) * HEAD, HEAD), HEAD)],
+                kv_ref.at[slot, side, pl.ds(j * d, d)],
+                kv_sem.at[slot, side, j],
+            )
+            for side, hbm in enumerate((w_gate_hbm, w_up_hbm))
+            for j in range(2)
         ]
 
     def wq_copies():
@@ -115,20 +135,18 @@
     def start_weights(u):
         slot = lax.rem(u, W_SLOTS)
 
-        @pl.when(u < ups)
-        def _():
-            start(up_copies(u, slot))
-
-        @pl.when((u >= ups) & (u < ups + downs))
-        def _():
-            start(down_copies(u - ups, slot))
+        @pl.when(u < ups - EARLY)
+        def _():
+            start(up_copies(EARLY + u, slot))
+
+        @pl.when((u >= ups - EARLY) & (u < ups - EARLY + downs))
+        def _():
+            start(down_copies(u - (ups - EARLY), slot))
 
     x_copy = pltpu.make_async_copy(x_hbm, x_ref, x_sem)
     x_copy.start()
     start(wq_copies())
-    for i in range(KV_SLOTS):
-        start(kv_copies(i, i))
-    start(wo_copies())
+    start(kv_copies(0, 0))
 
     barrier = pltpu.get_barrier_semaphore()
     for other in [partner] + [peer(r) for r in range(1, LINE)]:
@@ -146,11 +164,14 @@
         for j in range(d // part):
             columns = pl.ds(j * part, part)
             wide = src[rows, columns].astype(F32)
-            normed_ref[rows, columns] = (wide * scale * gain[:, columns].astype(F32)).astype(BF16)
+            normed_ref[rows, columns] = (wide * scale * gain[columns].astype(F32).reshape(1, part)).astype(BF16)
 
     x_copy.wait()
     for c in range(chunks):
         norm_rows(x_ref, pl.ds(c * ROWS, ROWS), gain_a_ref)
+    for i in range(1, KV_SLOTS):
+        start(kv_copies(i, i))
+    start(wo_copies())
     wait(wq_copies())
     cos, sin = turn_ref[0:1, :], turn_ref[1:2, :]
     q_ref[...] = jnp.zeros_like(q_ref)
@@ -172,7 +193,7 @@
         )
 
     class Sum:
-        def __init__(self, c, sems, pair_out, pair_in, line_out, line_in, part_of, block_of):
+        def __init__(self, c, sems, pair_out, pair_in, line_in, part_of, block_of):
             def one(src, dst, place, other):
                 return remote(src, dst, sems.at[c, 0, place], sems.at[c, 1, place], other)
 
@@ -181,7 +202,7 @@
 
             steps = range(1, LINE)
             self.pair = lambda: [one(pair_out.at[c], pair_in.at[c], 0, partner)]
-            self.line = lambda: [one(part_of(line_out, at_z(r)), line_in.at[c, r - 1], r, peer(r)) for r in steps]
+            self.line = lambda: [one(part_of(pair_in, at_z(r)), line_in.at[c, r - 1], r, peer(r)) for r in steps]
             self.gather = lambda: [gathered(z, 3 + r, peer(r)) for r in steps]
             self.own = lambda: [gathered(z, 7, partner)]
             self.passed = lambda: [gathered(at_z(LINE - r), 7 + r, partner) for r in steps]
@@ -218,13 +239,15 @@
         def block_of(place):
             return h_ref.at[rows, pl.ds(aligned(core * half_d + place * part_d, part_d), part_d)]
 
-        return Sum(c, sum1_sem, pair_out1, pair_in1, line_out1, line_in1, part_of, block_of)
+        return Sum(c, sum1_sem, pair_out1, pair_in1, line_in1, part_of, block_of)
 
     def add_pair1(c):
         def add():
             for j in range(half_d // part):
                 columns = pl.ds(j * part, part)
-                line_out1[c, :, columns] = (own1[c, :, columns] + pair_in1[c, :, columns].astype(F32)).astype(BF16)
+                both = own1[c, :, columns] + pair_in1[c, :, columns].astype(F32)
+                own1[c, :, columns] = both
+                pair_in1[c, :, columns] = both.astype(BF16)
 
         return add
 
@@ -233,30 +256,37 @@
             rows = pl.ds(aligned(c * ROWS, ROWS), ROWS)
             mine = pl.ds(aligned(z * part_d, part_d), part_d)
             columns = pl.ds(aligned(core * half_d + z * part_d, part_d), part_d)
-            total = own1[c, :, mine] + pair_in1[c, :, mine].astype(F32)
+            total = own1[c, :, mine]
             for r in range(LINE - 1):
                 total += line_in1[c, r].astype(F32)
             h_ref[rows, columns] = (x_ref[rows, columns].astype(F32) + total).astype(BF16)
 
         return add
 
+    def side_by_side(slot, which, at, rows):
+        return jnp.concatenate([kv_ref[slot, which, at : at + rows], kv_ref[slot, which, at + rows : at + 2 * rows]], 1)
+
     scaling = HEAD**-0.5
 
     def attend(i, slot):
+        def rows(s):
+            return pl.ds(aligned((i * SEQS + s) * 2 * heads, 2 * heads), 2 * heads)
+
+        def halves(which, s):
+            return side_by_side(slot, which, s * cache, half_cache)
+
+        scores, weights = [], []
         for s in range(SEQS):
-            at = pl.ds(aligned((i * SEQS + s) * 2 * heads, 2 * heads), 2 * heads)
-            q = jnp.concatenate([q_ref[0, at, :], q_ref[1, at, :]], 1).astype(BF16)
-            keys = jnp.concatenate([kv_ref[slot, 0, s, 0:half_cache], kv_ref[slot, 0, s, half_cache:cache]], 1)
-            scores = lax.dot_general(q, keys, (((1,), (1,)), ((), ())), preferred_element_type=F32) * scaling
-            top = jnp.max(scores, 1, keepdims=True)
-            top = jnp.maximum(top, pltpu.roll(top, heads, 0))
-            e = jnp.exp(scores - top)
+            q = jnp.concatenate([q_ref[0, rows(s), :], q_ref[1, rows(s), :]], 1).astype(BF16)
+            scores.append(lax.dot_general(q, halves(0, s), (((1,), (1,)), ((), ())), preferred_element_type=F32) * scaling)
+        for s in range(SEQS):
+            top = jnp.max(scores[s], 1, keepdims=True)
+            e = jnp.exp(scores[s] - jnp.maximum(top, pltpu.roll(top, heads, 0)))
             total = jnp.sum(e, 1, keepdims=True)
-            total = total + pltpu.roll(total, heads, 0)
-            weights = (e * (1.0 / total)).astype(BF16)
-            values = jnp.concatenate([kv_ref[slot, 1, s, 0:half_cache], kv_ref[slot, 1, s, half_cache:cache]], 1)
-            both = jnp.dot(weights, values, preferred_element_type=F32)
-            seen_ref[at, :] = both[:, 0:HEAD] + pltpu.roll(both[:, HEAD : 2 * HEAD], heads, 0)
+            weights.append((e * (1.0 / (total + pltpu.roll(total, heads, 0)))).astype(BF16))
+        for s in range(SEQS):
+            both = jnp.dot(weights[s], halves(1, s), preferred_element_type=F32)
+            seen_ref[rows(s), :] = both[:, 0:HEAD] + pltpu.roll(both[:, HEAD : 2 * HEAD], heads, 0)
 
     def project(c):
         seen = jnp.concatenate(
@@ -280,18 +310,13 @@
         def _():
             start(kv_copies(i + KV_SLOTS, slot))
 
-        @pl.when(i == steps - KV_SLOTS)
-        def _():
-            start_weights(0)
-
-        @pl.when(i == steps - KV_SLOTS + 1)
-        def _():
-            start_weights(1)
-            start_weights(2)
-
-        @pl.when(i == steps - KV_SLOTS + 2)
-        def _():
-            for u in range(3, W_SLOTS - 1):
+        @pl.when(i >= steps - EARLY)
+        def _():
+            start(early_copies(i - (steps - EARLY)))
+
+        @pl.when(i == steps - 1)
+        def _():
+            for u in range(W_SLOTS - 1):
                 start_weights(u)
 
         @pl.when((place == 0) & (i >= per_chunk))
@@ -330,14 +355,23 @@
     sum1(last).finish()
     norm_rows(h_ref, pl.ds(last * ROWS, ROWS), gain_m_ref)
 
-    @pl.loop(0, ups)
+    def gated(u, w_gate, w_up):
+        b = normed_ref[...]
+        gate = jnp.dot(b, w_gate, preferred_element_type=F32)
+        up = jnp.dot(b, w_up, preferred_element_type=F32)
+        hidden_ref[:, pl.ds(aligned(u * WIDE, WIDE), WIDE)] = (gate * (1.0 / (1.0 + jnp.exp(-gate))) * up).astype(BF16)
+
+    @pl.loop(0, EARLY)
+    def _(u):
+        slot = lax.rem(u + steps - EARLY, KV_SLOTS)
+        wait(early_copies(u))
+        gated(u, side_by_side(slot, 0, 0, d), side_by_side(slot, 1, 0, d))
+
+    @pl.loop(0, ups - EARLY)
     def _(u):
         slot = lax.rem(u, W_SLOTS)
-        wait(up_copies(u, slot))
-        b = normed_ref[...]
-        gate = jnp.dot(b, w_ref[slot, 0, 0:d], preferred_element_type=F32)
-        up = jnp.dot(b, w_ref[slot, 1, 0:d], preferred_element_type=F32)
-        hidden_ref[:, pl.ds(aligned(u * WIDE, WIDE), WIDE)] = (gate * (1.0 / (1.0 + jnp.exp(-gate))) * up).astype(BF16)
+        wait(up_copies(EARLY + u, slot))
+        gated(EARLY + u, w_ref[slot, 0, 0:d], w_ref[slot, 1, 0:d])
         start_weights(u + W_SLOTS)
 
     def sum2(n):
@@ -348,11 +382,13 @@
             columns = pl.ds(aligned((2 * n + core) * WIDE, WIDE), WIDE)
             return y_ref.at[pl.ds(aligned(place * row_part, row_part), row_part), columns]
 
-        return Sum(n, sum2_sem, pair_out2, pair_in2, line_out2, line_in2, part_of, block_of)
+        return Sum(n, sum2_sem, pair_out2, pair_in2, line_in2, part_of, block_of)
 
     def add_pair2(n):
         def add():
-            line_out2[n] = (own2[n] + pair_in2[n].astype(F32)).astype(BF16)
+            both = own2[n] + pair_in2[n].astype(F32)
+            own2[n] = both
+            pair_in2[n] = both.astype(BF16)
 
         return add
 
@@ -360,26 +396,26 @@
         def add():
             rows = pl.ds(aligned(z * row_part, row_part), row_part)
             columns = pl.ds(aligned((2 * n + core) * WIDE, WIDE), WIDE)
-            total = own2[n, rows] + pair_in2[n, rows].astype(F32)
+            total = own2[n, rows]
             for r in range(LINE - 1):
                 total += line_in2[n, r].astype(F32)
             y_ref[rows, columns] = (h_ref[rows, columns].astype(F32) + total).astype(BF16)
 
         return add
 
-    lag_line, lag_gather, lag_pass = 1, 4, 7
-
-    @pl.loop(0, downs + lag_pass)
+    lag_line, lag_gather, lag_pass, lag_end = LAGS
+
+    @pl.loop(0, downs + lag_end)
     def _(t):
         @pl.when(t < downs)
         def _():
-            slot = lax.rem(ups + t, W_SLOTS)
+            slot = lax.rem(ups - EARLY + t, W_SLOTS)
             wait(down_copies(t, slot))
             hidden = hidden_ref[...]
             own2[t] = jnp.dot(hidden, w_ref[slot, core, 0:ff], preferred_element_type=F32)
             pair_out2[t] = jnp.dot(hidden, w_ref[slot, 1 - core, 0:ff], preferred_element_type=F32).astype(BF16)
             sum2(t).send_pair()
-            start_weights(ups + t + W_SLOTS)
+            start_weights(ups - EARLY + t + W_SLOTS)
 
         @pl.when((t >= lag_line) & (t < downs + lag_line))
         def _():
@@ -389,17 +425,13 @@
         def _():
             sum2(t - lag_gather).send_gather(add_line2(t - lag_gather))
 
-        @pl.when(t >= lag_pass)
+        @pl.when((t >= lag_pass) & (t < downs + lag_pass))
         def _():
             sum2(t - lag_pass).pass_on()
 
-    @pl.loop(0, downs)
-    def _(n):
-        sum2(n).finish()
-
-    y_copy = pltpu.make_async_copy(y_ref, y_hbm, y_sem)
-    y_copy.start()
-    y_copy.wait()
+        @pl.when(t >= lag_end)
+        def _():
+            sum2(t - lag_end).finish()
 
 
 def solution(mesh):
@@ -419,46 +451,42 @@
         return pl.pallas_call(
             kernel,
             name="decoder_layer",
-            out_shape=jax.ShapeDtypeStruct(x.shape, BF16),
+            out_shape=pltpu.VMEM(x.shape, BF16),
             in_specs=[anywhere, anywhere, anywhere, vmem, anywhere, anywhere, vmem, anywhere, anywhere, anywhere, vmem],
-            out_specs=anywhere,
+            out_specs=vmem,
             scratch_shapes=[
-                pltpu.VMEM(x.shape, BF16),
                 pltpu.VMEM(x.shape, BF16),
                 pltpu.VMEM(x.shape, BF16),
                 pltpu.VMEM(x.shape, BF16),
                 pltpu.VMEM((batch, ff), BF16),
                 pltpu.VMEM((2, batch * 2 * heads, HEAD), F32),
                 pltpu.VMEM((batch * 2 * heads, HEAD), F32),
-                pltpu.VMEM((KV_SLOTS, 2, SEQS, cache, HEAD), BF16),
+                pltpu.VMEM((KV_SLOTS, 2, SEQS * cache, HEAD), BF16),
                 pltpu.VMEM((W_SLOTS, 2, max(d, ff), WIDE), BF16),
                 pltpu.VMEM((chunks, ROWS, half_d), F32),
-                pltpu.VMEM((chunks, ROWS, half_d), BF16),
                 pltpu.VMEM((chunks, ROWS, half_d), BF16),
                 pltpu.VMEM((chunks, ROWS, half_d), BF16),
                 pltpu.VMEM((chunks, LINE - 1, ROWS, part_d), BF16),
                 pltpu.VMEM((downs, batch, WIDE), F32),
                 pltpu.VMEM((downs, batch, WIDE), BF16),
                 pltpu.VMEM((downs, batch, WIDE), BF16),
-                pltpu.VMEM((downs, batch, WIDE), BF16),
                 pltpu.VMEM((downs, LINE - 1, row_part, WIDE), BF16),
                 dma,
-                dma((KV_SLOTS, 2)),
+                dma((KV_SLOTS, 2, max(2, KV_CUTS))),
                 dma((W_SLOTS, 2)),
                 dma((2, half_d // WIDE)),
-                dma,
                 dma((chunks, 2, 11)),
                 dma((downs, 2, 11)),
             ],
-            compiler_params=pltpu.CompilerParams(collective_id=0, has_side_effects=True, vmem_limit_bytes=67043328),
+            compiler_params=pltpu.CompilerParams(collective_id=0, has_side_effects=True, vmem_limit_bytes=66200000),
         )(
             x,
-            k_cache.reshape(batch, cache, HEAD),
-            v_cache.reshape(batch, cache, HEAD),
-            gain_a.reshape(1, d),
+            k_cache.reshape(batch * cache, HEAD),
+            v_cache.reshape(batch * cache, HEAD),
+            gain_a,
             wq,
             wo,
-            gain_m.reshape(1, d),
+            gain_m,
             w_gate,
             w_up,
             w_down,

time: 133 us -> 103 us (0.77)
  Pallas kernels: 128 us -> 102 us
  local copies, waits for them, and re-layouts: 4.6 us -> 0.84 us
    pallas_call x1, Pallas kernels: 128 us -> 102 us  [step(): pl.pallas_call(kernel, name='decoder_layer', out_shape=pltpu.VMEM(x.shape...]
    reshape x2 -> x0, local copies, waits for them, and re-layouts: 2.63 us -> none  [the longest x1 1.32 us: step(): gain_a.reshape(1, d)]
where the time goes in v2:
time: 103 us
  Pallas kernels  102 us (99%)
    pallas_call x1, Pallas kernels, step(): pl.pallas_call(kernel, name='decoder_layer', out_shape=pltpu.VMEM(x.shape...  102 us

profile of v2, /device:TPU:0, one launch (start us, length us, event | category | flops | bytes accessed | tf_op | source)
XLA Modules:
  0.0 102.5 jit_solution(6957024290102000165)
XLA Ops:
  0.0 101.7 %decoder_layer.1 = bf16[64,5120]{1,0:T(8,128)(2,1)S(1)} custom-call(bf16[64,5120]{1,0:T(8,128)(2,1)} %x_hbm.1, bf16[262144,128]{1,0:T(8,128)(2,1)} %bitcast.k_hbm, bf16[262144,128]{1,0:T(8,128)(2,1)} %bitcast.1.v_hbm, bf16[5120]{0:T(1024)(128)(2,1)} %gain_a_ref.1, bf16[5120,512]{1,0:T(8,128)(2,1)} %wq_hbm.1, bf16[512,5120]{1,0:T(8,128)(2,1)} %wo_hbm.1, ...), custom_call_target="tpu_custom_call" | custom-call | tf_op jit(solution)/shard_map/decoder_layer/pallas_call | solution.py:451
  101.7 0.8 copy.13

commit v3 on v2

--- a/solution.py
+++ b/solution.py
@@ -26,9 +26,9 @@
 
 
 def kernel(
-    x_hbm, k_hbm, v_hbm, gain_a_ref, wq_hbm, wo_hbm, gain_m_ref, w_gate_hbm, w_up_hbm, w_down_hbm, turn_ref,
+    x_hbm, k_hbm, v_hbm, gain_a_hbm, wq_hbm, wo_hbm, gain_m_hbm, w_gate_hbm, w_up_hbm, w_down_hbm, turn_hbm,
     y_ref,
-    x_ref, normed_ref, h_ref, hidden_ref, q_ref, seen_ref, kv_ref, w_ref,
+    x_ref, gain_a_ref, gain_m_ref, turn_ref, normed_ref, h_ref, hidden_ref, q_ref, seen_ref, kv_ref, w_ref,
     own1, pair_out1, pair_in1, line_in1,
     own2, pair_out2, pair_in2, line_in2,
     x_sem, kv_sem, w_sem, wo_sem, sum1_sem, sum2_sem,
@@ -143,8 +143,13 @@
         def _():
             start(down_copies(u - (ups - EARLY), slot))
 
-    x_copy = pltpu.make_async_copy(x_hbm, x_ref, x_sem)
-    x_copy.start()
+    small_copies = [
+        pltpu.make_async_copy(src, dst, x_sem.at[n])
+        for n, (src, dst) in enumerate(
+            ((x_hbm, x_ref), (gain_a_hbm, gain_a_ref), (gain_m_hbm, gain_m_ref), (turn_hbm, turn_ref))
+        )
+    ]
+    start(small_copies)
     start(wq_copies())
     start(kv_copies(0, 0))
 
@@ -166,7 +171,7 @@
             wide = src[rows, columns].astype(F32)
             normed_ref[rows, columns] = (wide * scale * gain[columns].astype(F32).reshape(1, part)).astype(BF16)
 
-    x_copy.wait()
+    wait(small_copies)
     for c in range(chunks):
         norm_rows(x_ref, pl.ds(c * ROWS, ROWS), gain_a_ref)
     for i in range(1, KV_SLOTS):
@@ -361,18 +366,18 @@
         up = jnp.dot(b, w_up, preferred_element_type=F32)
         hidden_ref[:, pl.ds(aligned(u * WIDE, WIDE), WIDE)] = (gate * (1.0 / (1.0 + jnp.exp(-gate))) * up).astype(BF16)
 
-    @pl.loop(0, EARLY)
-    def _(u):
-        slot = lax.rem(u + steps - EARLY, KV_SLOTS)
-        wait(early_copies(u))
-        gated(u, side_by_side(slot, 0, 0, d), side_by_side(slot, 1, 0, d))
-
     @pl.loop(0, ups - EARLY)
     def _(u):
         slot = lax.rem(u, W_SLOTS)
         wait(up_copies(EARLY + u, slot))
         gated(EARLY + u, w_ref[slot, 0, 0:d], w_ref[slot, 1, 0:d])
         start_weights(u + W_SLOTS)
+
+    @pl.loop(0, EARLY)
+    def _(u):
+        slot = lax.rem(u + steps - EARLY, KV_SLOTS)
+        wait(early_copies(u))
+        gated(u, side_by_side(slot, 0, 0, d), side_by_side(slot, 1, 0, d))
 
     def sum2(n):
         def part_of(ref, place):
@@ -452,10 +457,13 @@
             kernel,
             name="decoder_layer",
             out_shape=pltpu.VMEM(x.shape, BF16),
-            in_specs=[anywhere, anywhere, anywhere, vmem, anywhere, anywhere, vmem, anywhere, anywhere, anywhere, vmem],
+            in_specs=[anywhere] * 11,
             out_specs=vmem,
             scratch_shapes=[
                 pltpu.VMEM(x.shape, BF16),
+                pltpu.VMEM((d,), BF16),
+                pltpu.VMEM((d,), BF16),
+                pltpu.VMEM(turn.shape, F32),
                 pltpu.VMEM(x.shape, BF16),
                 pltpu.VMEM(x.shape, BF16),
                 pltpu.VMEM((batch, ff), BF16),
@@ -471,7 +479,7 @@
                 pltpu.VMEM((downs, batch, WIDE), BF16),
                 pltpu.VMEM((downs, batch, WIDE), BF16),
                 pltpu.VMEM((downs, LINE - 1, row_part, WIDE), BF16),
-                dma,
+                dma((4,)),
                 dma((KV_SLOTS, 2, max(2, KV_CUTS))),
                 dma((W_SLOTS, 2)),
                 dma((2, half_d // WIDE)),

time: 103 us -> 101 us (0.981)
  Pallas kernels: 102 us -> 99.6 us
    pallas_call x1, Pallas kernels: 102 us -> 99.6 us  [step(): pl.pallas_call(kernel, name='decoder_layer', out_shape=pltpu.VMEM(x.shape...]
where the time goes in v3:
time: 101 us; the launch traced here: 100 us
  Pallas kernels  99.6 us (99%)
    pallas_call x1, Pallas kernels, step(): pl.pallas_call(kernel, name='decoder_layer', out_shape=pltpu.VMEM(x.shape...  99.6 us

profile of v3, /device:TPU:0, one launch (start us, length us, event | category | flops | bytes accessed | tf_op | source)
XLA Modules:
  0.0 100.5 jit_solution(12206943908945848605)
XLA Ops:
  0.0 99.6 %decoder_layer.1 = bf16[64,5120]{1,0:T(8,128)(2,1)S(1)} custom-call(bf16[64,5120]{1,0:T(8,128)(2,1)} %x_hbm.1, bf16[262144,128]{1,0:T(8,128)(2,1)} %bitcast.k_hbm, bf16[262144,128]{1,0:T(8,128)(2,1)} %bitcast.1.v_hbm, bf16[5120]{0:T(1024)(128)(2,1)} %gain_a_hbm.1, bf16[5120,512]{1,0:T(8,128)(2,1)} %wq_hbm.1, bf16[512,5120]{1,0:T(8,128)(2,1)} %wo_hbm.1, ...), custom_call_target="tpu_custom_call" | custom-call | tf_op jit(solution)/shard_map/decoder_layer/pallas_call | solution.py:456
  99.6 0.8 copy.13
